TPU v7x, 32 devices: a whole 2x2x4 slice. The times are simulated.
32 devices in a mesh: tm: 8 (over z, x), pair: 4 (over y, core).
Axes of the slice: x: 2, y: 2, z: 4, core: 2. Of those that a mesh axis runs over, the one named last changes fastest.
Arguments:
- voltages: bfloat16 [2, 32, 262144], P(None, 'pair', 'tm'), may hold values from -3 to 3
- delays: int32 [32, 32], P('pair', 'tm'), may hold values from 0 to 49152, as said below
- phase_model: float32 [32, 8192], replicated, may hold values from -3.140625 to 3.140625
- phase_bins: int32 [32], P('tm'), may hold values from 0 to 31
- assignment: int32 [16], P('pair'), may hold values from 0 to 15, each once
Outputs:
- visibility: float32 [32, 16, 2, 64, 128], P('tm', 'pair')
Inputs may be any that keep to these rules, and one draw needn't show every extreme that they name: `delays`: delay of each station in each recording block of 1 frames; both 0 and 49152 occur in every draw. `assignment`: each of the 16 station-pair blocks occurs once.
All inputs are finite; a program needn't handle non-finite values.
Results may differ from a plain program's by a relative error of at most 0.0085.
Values may be sent and summed in bfloat16 or wider, within the bound.
A program may use at most 128 MiB of HBM per device.

v0:
```python
import math

import jax
import jax.numpy as jnp
from jax import lax
from jax.sharding import PartitionSpec as P

NCHAN = 8192
GROUP_ST = 8
RADIX_A = 16
CHAVG = 64
BINS = 32
TBLK = 4
FB = 1
NGRP = 4
OUTCH = 128


def from_behind(value, axis, steps):
    count = lax.axis_size(axis)
    first, last = (max(0, -steps), min(count, count - steps))
    return lax.ppermute(value, axis, [(source, source + steps) for source in range(first, last)])


def dft_tables(radix_small, radix_large):
    index_small = jnp.arange(radix_small, dtype=jnp.int32)
    index_large = jnp.arange(radix_large, dtype=jnp.int32)
    small_turns = index_small[:, None] * index_small[None, :] % radix_small
    small_angle = small_turns.astype(jnp.float32) * (2.0 * math.pi / radix_small)
    small_scale = 1.0 / math.sqrt(radix_small)
    small_cos = (jnp.cos(small_angle) * small_scale).astype(jnp.bfloat16)
    small_sin = (jnp.sin(small_angle) * small_scale).astype(jnp.bfloat16)
    twist_turns = index_small[:, None] * index_large[None, :]
    twist_angle = twist_turns.astype(jnp.float32) * (2.0 * math.pi / (radix_small * radix_large))
    twist_cos = jnp.cos(twist_angle)
    twist_sin = jnp.sin(twist_angle)
    large_turns = index_large[:, None] * index_large[None, :] % radix_large
    large_angle = large_turns.astype(jnp.float32) * (2.0 * math.pi / radix_large)
    large_scale = 1.0 / math.sqrt(radix_large)
    large_cos = (jnp.cos(large_angle) * large_scale).astype(jnp.bfloat16)
    large_sin = (jnp.sin(large_angle) * large_scale).astype(jnp.bfloat16)
    return (small_cos, small_sin, twist_cos, twist_sin, large_cos, large_sin)


def reorder_last(table):
    lead = table.shape[:-1]
    radix_large = table.shape[-1]
    group_width = radix_large // OUTCH
    moved = table.reshape(lead + (OUTCH, group_width))
    moved = jnp.swapaxes(moved, -1, -2)
    return moved.reshape(lead + (radix_large,))


def section_tables(radix_small, radix_large):
    small_cos, small_sin, twist_cos, twist_sin, large_cos, large_sin = dft_tables(
        radix_small, radix_large
    )
    large_cos = reorder_last(large_cos)
    large_sin = reorder_last(large_sin)
    first_table = jnp.stack(
        [jnp.stack([small_cos, small_sin], 1), jnp.stack([-small_sin, small_cos], 1)], 0
    )
    second_table = jnp.concatenate(
        [jnp.concatenate([large_cos, -large_sin], 1), jnp.concatenate([large_sin, large_cos], 1)], 0
    )
    return (first_table, twist_cos, twist_sin, second_table)


def channelize(windows, phase_cos, phase_sin, tables):
    first_table, twist_cos, twist_sin, second_table = tables
    first_pass = jnp.einsum(
        "pkrn,rsfnm->sfkpm", first_table, windows, preferred_element_type=jnp.float32
    )
    real_part = first_pass[:, :, :, 0]
    imag_part = first_pass[:, :, :, 1]
    turned = jnp.stack(
        [
            real_part * twist_cos + imag_part * twist_sin,
            imag_part * twist_cos - real_part * twist_sin,
        ],
        3,
    ).astype(jnp.bfloat16)
    turned_shape = turned.shape
    channels = jnp.dot(
        turned.reshape(-1, second_table.shape[0]), second_table, preferred_element_type=jnp.float32
    ).reshape(turned_shape)
    real_part = channels[:, :, :, 0]
    imag_part = channels[:, :, :, 1]
    phase_re = phase_cos[:, None]
    phase_im = phase_sin[:, None]
    return jnp.stack(
        [real_part * phase_re - imag_part * phase_im, real_part * phase_im + imag_part * phase_re],
        3,
    ).astype(jnp.bfloat16)


def slot_products(spectra, block):
    grouped = spectra.reshape(spectra.shape[0], spectra.shape[1], spectra.shape[2], 2, -1, OUTCH)
    row_start = block // NGRP * GROUP_ST
    col_start = block % NGRP * GROUP_ST
    left_block = lax.dynamic_slice_in_dim(grouped, row_start, GROUP_ST, 0)
    right_block = lax.dynamic_slice_in_dim(grouped, col_start, GROUP_ST, 0)
    gram_terms = jnp.einsum(
        "ifargo,jfasgo->firjso", left_block, right_block, preferred_element_type=jnp.float32
    )
    real_part = gram_terms[:, :, 0, :, 0] + gram_terms[:, :, 1, :, 1]
    imag_part = gram_terms[:, :, 1, :, 0] - gram_terms[:, :, 0, :, 1]
    paired = jnp.stack([real_part, imag_part], 1)
    return paired.reshape(paired.shape[0], 2, GROUP_ST * GROUP_ST, OUTCH) * (1.0 / CHAVG)


def body(voltages, delays, phase_model, phase_bins, assignment):
    local_stations = voltages.shape[1]
    radix_large = NCHAN // RADIX_A
    tables = section_tables(RADIX_A, radix_large)
    following = from_behind(voltages, "tm", -1)
    beyond = from_behind(voltages, "tm", -2)
    extended = jnp.concatenate([voltages, following, beyond], 2)
    angles = phase_model.reshape(phase_model.shape[0], radix_large, RADIX_A).transpose(0, 2, 1)
    angles = reorder_last(angles)
    angles = lax.dynamic_slice_in_dim(
        angles, lax.axis_index("pair") * local_stations, local_stations, 0
    )
    phase_cos = jnp.cos(angles)
    phase_sin = jnp.sin(angles)
    frame_span = FB * NCHAN

    def cut(series, offset):
        return lax.dynamic_slice_in_dim(series, offset, frame_span, 1)

    pieces = []
    for segment in range(TBLK):
        offsets = segment * frame_span + delays[:, segment]
        windows = jax.vmap(cut, in_axes=(1, 0), out_axes=1)(extended, offsets)
        windows = windows.reshape(2, local_stations, FB, RADIX_A, radix_large)
        local_spectra = channelize(windows, phase_cos, phase_sin, tables)
        spectra = lax.all_gather(local_spectra, "pair", axis=0, tiled=True)

        def one_slot(block):
            return slot_products(spectra, block)

        slot_terms = jax.vmap(one_slot, out_axes=1)(assignment)
        pieces.append(slot_terms.reshape(FB, -1))
    products = jnp.concatenate(pieces, 0)
    bin_index = jnp.arange(BINS, dtype=jnp.int32)
    bins_here = BINS // lax.axis_size("tm")
    out_shape = (bins_here, assignment.shape[0], 2, GROUP_ST * GROUP_ST, OUTCH)
    slices = lax.axis_size("tm")
    width = products.shape[1] // slices
    routed = lax.all_to_all(
        products.reshape(products.shape[0], slices, width).astype(jnp.bfloat16),
        "tm",
        split_axis=1,
        concat_axis=0,
        tiled=True,
    ).astype(jnp.float32)
    every_bin = lax.all_gather(phase_bins, "tm", axis=0, tiled=True)
    onehot_all = (every_bin[:, None] == bin_index[None, :]).astype(jnp.float32)
    partial_value = jnp.dot(
        onehot_all.T, routed.reshape(routed.shape[0], width), precision=lax.Precision.HIGHEST
    )
    returned = lax.all_to_all(
        partial_value.reshape(BINS, 1, width), "tm", split_axis=0, concat_axis=1, tiled=True
    )
    held_bins = returned.reshape(bins_here, slices * width)
    return held_bins.reshape(out_shape)


def solution(mesh):
    in_specs = (P(None, "pair", "tm"), P("pair", "tm"), P(), P("tm"), P("pair"))
    out_specs = P("tm", "pair", None, None, None)
    return jax.shard_map(body, mesh=mesh, in_specs=in_specs, out_specs=out_specs, check_vma=False)
```

profile of v0, /device:TPU:0, one launch (start us, length us, event | category | flops | bytes accessed | tf_op | source)
XLA Modules:
  0.0 625.5 jit_solution(6308306107612617593)
XLA Ops:
  6.5 2.3 copy.113
  12.4 3.6 copy.116
  16.1 4.2 copy.117
  22.5 4.3 fusion.15
  26.7 4.9 multiply_convert_fusion
  32.0 5.0 collective-permute-done
  37.0 23.6 %collective-permute-done.1 = bf16[2,8,32768]{2,0,1:T(2,128)(2,1)} collective-permute-done((bf16[2,8,32768]{2,0,1:T(2,128)(2,1)S(1)}, bf16[2,8,32768]{2,0,1:T(2,128)(2,1)}, u32[]{:S(2)}, u32[]{:S(2)}) %collective-permute-start.1) | collective-permute-done | bytes 1048608 | tf_op jit(solution)/shard_map/ppermute | solution.py:22
  60.6 11.9 %maximum_bitcast_fusion = bf16[8,2,98304]{2,1,0:T(2,128)(2,1)} fusion(bf16[2,8,32768]{2,0,1:T(2,128)(2,1)} %collective-permute-done.1, bf16[2,8,32768]{2,0,1:T(2,128)(2,1)} %collective-permute-done, bf16[2,8,32768]{2,0,1:T(2,128)(2,1)S(1)} %copy.113), kind=kLoop, calls=%fused_computation.21 | loop fusion | flops 9437184 | bytes 6291456 | tf_op jit(solution)/shard_map/vmap()/transpose | solution.py:129
  72.7 22.1 %while.5 = (s32[]{:T(128)}, bf16[8,2,98304]{2,1,0:T(2,128)(2,1)}, s32[8,3]{0,1:T(4,128)S(1)}, bf16[8,2,8192]{2,1,0:T(2,128)(2,1)S(1)}, s32[]{:T(128)}) while((s32[]{:T(128)}, bf16[8,2,98304]{2,1,0:T(2,128)(2,1)}, s32[8,3]{0,1:T(4,128)S(1)}, bf16[8,2,8192]{2,1,0:T(2,128)(2,1)S(1)}, s32[]{:T(128)}) %tuple.99), condition=%wide.while_cond.1, body=%wide.while_body.1.sunk | while | flops 2 | bytes 65653 | solution.py:129
  73.3 2.1 dynamic-slice_dynamic-update-slice_fusion.9
  78.8 2.1 dynamic-slice_dynamic-update-slice_fusion.9
  81.6 2.1 dynamic-slice_dynamic-update-slice_fusion.9
  87.1 2.1 dynamic-slice_dynamic-update-slice_fusion.9
  89.9 2.1 dynamic-slice_dynamic-update-slice_fusion.9
  92.6 2.1 dynamic-slice_dynamic-update-slice_fusion.9
  95.1 22.1 %while.4 = (s32[]{:T(128)}, bf16[8,2,98304]{2,1,0:T(2,128)(2,1)}, s32[8,3]{0,1:T(4,128)S(1)}, bf16[8,2,8192]{2,1,0:T(2,128)(2,1)S(1)}, s32[]{:T(128)}) while((s32[]{:T(128)}, bf16[8,2,98304]{2,1,0:T(2,128)(2,1)}, s32[8,3]{0,1:T(4,128)S(1)}, bf16[8,2,8192]{2,1,0:T(2,128)(2,1)S(1)}, s32[]{:T(128)}) %tuple.116), condition=%wide.while_cond, body=%wide.while_body.sunk | while | flops 2 | bytes 65653 | solution.py:129
  98.5 2.1 dynamic-slice_dynamic-update-slice_fusion.8
  101.2 2.1 dynamic-slice_dynamic-update-slice_fusion.8
  109.5 2.1 dynamic-slice_dynamic-update-slice_fusion.8
  112.3 2.1 dynamic-slice_dynamic-update-slice_fusion.8
  118.1 22.1 %while.7 = (s32[]{:T(128)}, bf16[8,2,98304]{2,1,0:T(2,128)(2,1)}, s32[8,3]{0,1:T(4,128)S(1)}, bf16[8,2,8192]{2,1,0:T(2,128)(2,1)S(1)}, s32[]{:T(128)}) while((s32[]{:T(128)}, bf16[8,2,98304]{2,1,0:T(2,128)(2,1)}, s32[8,3]{0,1:T(4,128)S(1)}, bf16[8,2,8192]{2,1,0:T(2,128)(2,1)S(1)}, s32[]{:T(128)}) %tuple.117), condition=%wide.while_cond.3, body=%wide.while_body.3.sunk | while | flops 2 | bytes 65653 | solution.py:129
  124.2 2.1 dynamic-slice_dynamic-update-slice_fusion.11
  127.0 2.1 dynamic-slice_dynamic-update-slice_fusion.11
  132.5 2.1 dynamic-slice_dynamic-update-slice_fusion.11
  135.3 2.1 dynamic-slice_dynamic-update-slice_fusion.11
  138.0 2.1 dynamic-slice_dynamic-update-slice_fusion.11
  143.2 23.0 %while.6 = (s32[]{:T(128)}, bf16[8,2,98304]{2,1,0:T(2,128)(2,1)}, s32[8,3]{0,1:T(4,128)S(1)}, bf16[8,2,8192]{2,1,0:T(2,128)(2,1)S(1)}, s32[]{:T(128)}) while((s32[]{:T(128)}, bf16[8,2,98304]{2,1,0:T(2,128)(2,1)}, s32[8,3]{0,1:T(4,128)S(1)}, bf16[8,2,8192]{2,1,0:T(2,128)(2,1)S(1)}, s32[]{:T(128)}) %tuple.118), condition=%wide.while_cond.2, body=%wide.while_body.2.sunk | while | flops 2 | bytes 65653 | solution.py:129
  143.9 2.1 dynamic-slice_dynamic-update-slice_fusion.10
  146.7 2.1 dynamic-slice_dynamic-update-slice_fusion.10
  149.5 2.1 dynamic-slice_dynamic-update-slice_fusion.10
  152.3 2.1 dynamic-slice_dynamic-update-slice_fusion.10
  155.2 2.1 dynamic-slice_dynamic-update-slice_fusion.10
  158.0 2.1 dynamic-slice_dynamic-update-slice_fusion.10
  160.8 2.1 dynamic-slice_dynamic-update-slice_fusion.10
  163.6 2.2 dynamic-slice_dynamic-update-slice_fusion.10
  168.4 2.1 add_convert_fusion.7
  174.4 2.6 convolution_bitcast_fusion.9
  186.3 13.7 %all-gather.5.cloned.1.call-done = bf16[32,1,16,2,512]{4,2,0,3,1:T(8,128)(2,1)} async-done(((bf16[8,1,16,2,512]{4,2,0,3,1:T(8,128)(2,1)}), bf16[32,1,16,2,512]{4,2,0,3,1:T(8,128)(2,1)}) %all-gather.5.cloned.1.call-update) | async-done | bytes 1048592 | tf_op jit(solution)/shard_map/all_gather | solution.py:137
  203.9 14.3 %all-gather.7.cloned.1.call-done = bf16[32,1,16,2,512]{4,2,0,3,1:T(8,128)(2,1)} async-done(((bf16[8,1,16,2,512]{4,2,0,3,1:T(8,128)(2,1)}), bf16[32,1,16,2,512]{4,2,0,3,1:T(8,128)(2,1)}) %all-gather.7.cloned.1.call-update) | async-done | bytes 1048592 | tf_op jit(solution)/shard_map/all_gather | solution.py:137
  223.2 13.4 %all-gather.9.cloned.1.call-done = bf16[32,1,16,2,512]{4,2,0,3,1:T(8,128)(2,1)} async-done(((bf16[8,1,16,2,512]{4,2,0,3,1:T(8,128)(2,1)}), bf16[32,1,16,2,512]{4,2,0,3,1:T(8,128)(2,1)}) %all-gather.9.cloned.1.call-update) | async-done | bytes 1048592 | tf_op jit(solution)/shard_map/all_gather | solution.py:137
  241.4 13.3 %all-gather.11.cloned.1.call-done = bf16[32,1,16,2,512]{4,2,0,3,1:T(8,128)(2,1)} async-done(((bf16[8,1,16,2,512]{4,2,0,3,1:T(8,128)(2,1)}), bf16[32,1,16,2,512]{4,2,0,3,1:T(8,128)(2,1)}) %all-gather.11.cloned.1.call-update) | async-done | bytes 1048592 | tf_op jit(solution)/shard_map/all_gather | solution.py:137
  258.7 11.9 %copy.158 = bf16[4,8,16,2,4,128,1]{2,1,4,6,3,5,0:T(8,128)(2,1)} copy(bf16[4,8,16,2,4,128,1]{5,2,3,4,1,0,6:T(8,128)(2,1)S(1)} %bitcast.329) | data formatting | bytes 2097152 | tf_op jit(solution)/shard_map/vmap()/gather | solution.py:102
  270.6 11.8 %copy.159 = bf16[4,8,16,2,4,128,1]{2,1,4,3,6,5,0:T(8,128)(2,1)} copy(bf16[4,8,16,2,4,128,1]{5,2,3,4,1,0,6:T(8,128)(2,1)S(1)} %bitcast.330) | data formatting | bytes 2097152 | tf_op jit(solution)/shard_map/vmap()/gather | solution.py:101
  282.4 43.9 %convolution_bitcast_fusion.4 = f32[4,1,8,2,8,2,128]{2,4,3,5,6,0,1:T(8,128)} fusion(bf16[4,8,16,2,4,128,1]{2,1,4,6,3,5,0:T(8,128)(2,1)} %copy.158, bf16[4,8,16,2,4,128,1]{2,1,4,3,6,5,0:T(8,128)(2,1)} %copy.159), kind=kOutput, calls=%fused_computation.20 | convolution fusion | flops 16777216 | bytes 2621440 | tf_op jit(solution)/shard_map/vmap(ifargo,jfasgo->firjso)/dot_general | solution.py:103
  326.3 5.3 slice_add_fusion.3
  331.6 2.2 copy.122
  334.5 12.8 %copy.165 = bf16[4,8,16,2,4,128,1]{2,1,4,6,3,5,0:T(8,128)(2,1)} copy(bf16[4,8,16,2,4,128,1]{5,2,3,4,1,0,6:T(8,128)(2,1)} %bitcast.328) | data formatting | bytes 2097152 | tf_op jit(solution)/shard_map/vmap()/gather | solution.py:102
  347.4 11.8 %copy.166 = bf16[4,8,16,2,4,128,1]{2,1,4,3,6,5,0:T(8,128)(2,1)} copy(bf16[4,8,16,2,4,128,1]{5,2,3,4,1,0,6:T(8,128)(2,1)S(1)} %bitcast.327) | data formatting | bytes 2097152 | tf_op jit(solution)/shard_map/vmap()/gather | solution.py:101
  359.2 43.9 %convolution_bitcast_fusion.3 = f32[4,1,8,2,8,2,128]{2,4,3,5,6,0,1:T(8,128)} fusion(bf16[4,8,16,2,4,128,1]{2,1,4,6,3,5,0:T(8,128)(2,1)} %copy.165, bf16[4,8,16,2,4,128,1]{2,1,4,3,6,5,0:T(8,128)(2,1)} %copy.166), kind=kOutput, calls=%fused_computation.19 | convolution fusion | flops 16777216 | bytes 2621440 | tf_op jit(solution)/shard_map/vmap(ifargo,jfasgo->firjso)/dot_general | solution.py:103
  403.1 5.3 slice_add_fusion.2
  408.4 2.2 copy.131
  412.0 12.8 %copy.171 = bf16[4,8,16,2,4,128,1]{2,1,4,6,3,5,0:T(8,128)(2,1)} copy(bf16[4,8,16,2,4,128,1]{5,2,3,4,1,0,6:T(8,128)(2,1)} %bitcast.326) | data formatting | bytes 2097152 | tf_op jit(solution)/shard_map/vmap()/gather | solution.py:102
  424.8 11.8 %copy.172 = bf16[4,8,16,2,4,128,1]{2,1,4,3,6,5,0:T(8,128)(2,1)} copy(bf16[4,8,16,2,4,128,1]{5,2,3,4,1,0,6:T(8,128)(2,1)S(1)} %bitcast.325) | data formatting | bytes 2097152 | tf_op jit(solution)/shard_map/vmap()/gather | solution.py:101
  436.6 44.1 %convolution_bitcast_fusion.2 = f32[4,1,8,2,8,2,128]{2,4,3,5,6,0,1:T(8,128)} fusion(bf16[4,8,16,2,4,128,1]{2,1,4,6,3,5,0:T(8,128)(2,1)} %copy.171, bf16[4,8,16,2,4,128,1]{2,1,4,3,6,5,0:T(8,128)(2,1)} %copy.172), kind=kOutput, calls=%fused_computation.18 | convolution fusion | flops 16777216 | bytes 2621440 | tf_op jit(solution)/shard_map/vmap(ifargo,jfasgo->firjso)/dot_general | solution.py:103
  480.8 5.3 slice_add_fusion.1
  486.0 2.2 copy.140
  489.0 11.8 %copy.177 = bf16[4,8,16,2,4,128,1]{2,1,4,6,3,5,0:T(8,128)(2,1)} copy(bf16[4,8,16,2,4,128,1]{5,2,3,4,1,0,6:T(8,128)(2,1)S(1)} %bitcast.323) | data formatting | bytes 2097152 | tf_op jit(solution)/shard_map/vmap()/gather | solution.py:102
  500.8 11.8 %copy.178 = bf16[4,8,16,2,4,128,1]{2,1,4,3,6,5,0:T(8,128)(2,1)} copy(bf16[4,8,16,2,4,128,1]{5,2,3,4,1,0,6:T(8,128)(2,1)S(1)} %bitcast.324) | data formatting | bytes 2097152 | tf_op jit(solution)/shard_map/vmap()/gather | solution.py:101
  512.6 44.0 %convolution_bitcast_fusion.1 = f32[4,1,8,2,8,2,128]{2,4,3,5,6,0,1:T(8,128)} fusion(bf16[4,8,16,2,4,128,1]{2,1,4,6,3,5,0:T(8,128)(2,1)} %copy.177, bf16[4,8,16,2,4,128,1]{2,1,4,3,6,5,0:T(8,128)(2,1)} %copy.178), kind=kOutput, calls=%fused_computation.17 | convolution fusion | flops 16777216 | bytes 2621440 | tf_op jit(solution)/shard_map/vmap(ifargo,jfasgo->firjso)/dot_general | solution.py:103
  556.6 5.3 slice_add_fusion
  561.9 2.2 copy.149
  566.1 5.5 all-to-all-start
  573.2 13.7 %all-reduce.4 = s32[32]{0:T(128)S(1)} all-reduce(s32[32]{0:T(128)S(1)} %dynamic-update-slice.8), channel_id=1, replica_groups=mesh['tm'=8,'pair'=4] {'tm'}, use_global_device_ids=true, to_apply=%add.4 | all-reduce | flops 32 | bytes 256
  588.5 29.2 %all_to_all.30 = f32[32,1,8192]{2,1,0:T(1,128)S(1)} all-to-all(f32[32,1,8192]{2,1,0:T(1,128)S(1)} %copy.153), channel_id=1, replica_groups=mesh['tm'=8,'pair'=4] {'tm'}, dimensions={0} | all-to-all | bytes 2097152 | tf_op jit(solution)/shard_map/all_to_all | solution.py:162
  (194 shorter events, 90.8 us)
Async XLA Ops:
  6.5 193.4 %all-gather.5.cloned.1.call-start = ((), (), s32[]{:S(2)}) async-start(), calls=%async_computation.2 | async-start | bytes 1310720 | tf_op jit(solution)/shard_map/all_gather | solution.py:137
  8.8 28.1 %collective-permute-start = (bf16[2,8,32768]{2,0,1:T(2,128)(2,1)S(1)}, bf16[2,8,32768]{2,0,1:T(2,128)(2,1)}, u32[]{:S(2)}, u32[]{:S(2)}) collective-permute-start(bf16[2,8,32768]{2,0,1:T(2,128)(2,1)S(1)} %copy.113), channel_id=1, source_target_pairs={{4,0},{8,4},{12,8},{16,12},{20,16},{24,20},{28,24},{5,1},{9,5},{13... | collective-permute-start | bytes 3145736 | tf_op jit(solution)/shard_map/ppermute | solution.py:22
  10.1 50.5 %collective-permute-start.1 = (bf16[2,8,32768]{2,0,1:T(2,128)(2,1)S(1)}, bf16[2,8,32768]{2,0,1:T(2,128)(2,1)}, u32[]{:S(2)}, u32[]{:S(2)}) collective-permute-start(bf16[2,8,32768]{2,0,1:T(2,128)(2,1)S(1)} %copy.113), channel_id=1, source_target_pairs={{8,0},{12,4},{16,8},{20,12},{24,16},{28,20},{9,1},{13,5},{17,9},{2... | collective-permute-start | bytes 3145736 | tf_op jit(solution)/shard_map/ppermute | solution.py:22
  140.2 0.7 copy-start.6
  166.3 0.7 copy-start.5
  171.5 1.7 copy-start.7
  171.5 1.7 copy-start.8
  179.1 1.8 copy-start.4
  180.9 5.3 copy-start.10
  183.8 34.5 %all-gather.7.cloned.1.call-start = ((), (), s32[]{:S(2)}) async-start(), calls=%async_computation.3 | async-start | bytes 1310720 | tf_op jit(solution)/shard_map/all_gather | solution.py:137
  184.6 52.0 %all-gather.9.cloned.1.call-start = ((), (), s32[]{:S(2)}) async-start(), calls=%async_computation.4 | async-start | bytes 1310720 | tf_op jit(solution)/shard_map/all_gather | solution.py:137
  185.4 69.3 %all-gather.11.cloned.1.call-start = ((), (), s32[]{:S(2)}) async-start(), calls=%async_computation.5 | async-start | bytes 1310720 | tf_op jit(solution)/shard_map/all_gather | solution.py:137
  258.7 11.9 %copy-start.3 = (bf16[4,8,16,2,4,128]{5,2,3,4,1,0:T(8,128)(2,1)S(1)}, bf16[4,8,16,2,4,128]{5,2,3,4,1,0:T(8,128)(2,1)}, u32[]{:S(2)}) copy-start(bf16[4,8,16,2,4,128]{5,2,3,4,1,0:T(8,128)(2,1)} %gather_fusion.1) | copy-start | bytes 3145732
  334.5 12.9 %copy-start.2 = (bf16[4,8,16,2,4,128]{5,2,3,4,1,0:T(8,128)(2,1)S(1)}, bf16[4,8,16,2,4,128]{5,2,3,4,1,0:T(8,128)(2,1)}, u32[]{:S(2)}) copy-start(bf16[4,8,16,2,4,128]{5,2,3,4,1,0:T(8,128)(2,1)} %gather_fusion.3) | copy-start | bytes 3145732
  412.0 12.8 %copy-start.1 = (bf16[4,8,16,2,4,128]{5,2,3,4,1,0:T(8,128)(2,1)S(1)}, bf16[4,8,16,2,4,128]{5,2,3,4,1,0:T(8,128)(2,1)}, u32[]{:S(2)}) copy-start(bf16[4,8,16,2,4,128]{5,2,3,4,1,0:T(8,128)(2,1)} %gather_fusion.5) | copy-start | bytes 3145732
  489.0 11.8 %copy-start = (bf16[4,8,16,2,4,128]{5,2,3,4,1,0:T(8,128)(2,1)S(1)}, bf16[4,8,16,2,4,128]{5,2,3,4,1,0:T(8,128)(2,1)}, u32[]{:S(2)}) copy-start(bf16[4,8,16,2,4,128]{5,2,3,4,1,0:T(8,128)(2,1)} %gather_fusion.7) | copy-start | bytes 3145732
  561.9 3.0 copy-start.9
  564.1 7.6 %copy-start.12 = (u32[32]{0:T(128)S(1)}, u32[32]{0:T(128)}, u32[]{:S(2)}) copy-start(u32[32]{0:T(128)} %constant.563) | copy-start | bytes 388
  564.1 8.9 %copy-start.11 = (s32[4]{0:T(128)S(1)}, s32[4]{0:T(128)}, u32[]{:S(2)}) copy-start(s32[4]{0:T(128)} %param.8) | copy-start | bytes 52
  566.1 20.8 %all-to-all-start = ((bf16[4,8,8192]{2,0,1:T(4,128)(2,1)}), bf16[4,8,8192]{2,0,1:T(4,128)(2,1)S(1)}, u32[]{:S(2)}, u32[]{:S(2)}) async-start(bf16[4,8,8192]{2,0,1:T(4,128)(2,1)} %copy.152), calls=%async_computation | async-start | bytes 1048576 | tf_op jit(solution)/shard_map/all_to_all | solution.py:150
Sparse Core Ops, SparseCore 0:
  183.9 15.9 all-gather.4
  201.5 16.6 all-gather.6
  219.8 16.6 all-gather.8
  238.0 16.6 all-gather.10
where the time goes:
time: 636 us; the launch traced here: 625 us
  local copies, waits for them, and re-layouts  238 us (37%)
  matrix products  184 us (29%)
  waiting for transfers between devices  83.4 us (13%)
  other arithmetic  52.7 us (8%)
  blocking collectives  42.9 us (7%)
  between operations  14.6 us (2%)
  starting transfers between devices  8.22 us (1%)
    dot_general x4, matrix products, slot_products(): jnp.einsum('ifargo,jfasgo->firjso', left_block, right_block, preferred_el...  176 us
    gather x96, local copies, waits for them, and re-layouts  88.3 us
    all_gather x4, waiting for transfers between devices, body(): spectra = lax.all_gather(local_spectra, 'pair', axis=0, tiled=True)  54.7 us
    gather x8, local copies, waits for them, and re-layouts, slot_products(): right_block = lax.dynamic_slice_in_dim(grouped, col_start, GROUP_ST, 0)  54.2 us
    gather x8, local copies, waits for them, and re-layouts, slot_products(): left_block = lax.dynamic_slice_in_dim(grouped, row_start, GROUP_ST, 0)  54 us
    all_to_all x1, blocking collectives, body(): lax.all_to_all(partial_value.reshape(BINS, 1, width), 'tm', split_axis=0,...  29.2 us
    ppermute x2, waiting for transfers between devices, from_behind(): lax.ppermute(value, axis, [(source, source + steps) for source in range(f...  28.6 us
    add x4, other arithmetic, slot_products(): real_part = gram_terms[:, :, 0, :, 0] + gram_terms[:, :, 1, :, 1]  21.1 us
  transfers between devices with their start and end apart: 7, of which 6 were waited for; matrix products, arithmetic and copies ran while one was open for 6% of the time, Pallas kernels for 0%

commit v1 on v0

v1 whole, which is shorter than its diff:
```python
import functools
import math

import jax
import jax.numpy as jnp
import numpy as np
from jax import lax
from jax.experimental import pallas as pl
from jax.experimental.pallas import tpu as pltpu
from jax.sharding import PartitionSpec as P

NCHAN = 8192
GROUP_ST = 8
RADIX_A = 16
CHAVG = 64
NGRP = 4
OUTCH = 128
BINS = 32
DELAY_MAX = 49152
LANES = 128
RADIX_B = NCHAN // RADIX_A
QUADS = RADIX_B // LANES
F32, BF16 = jnp.float32, jnp.bfloat16
AXES = ("tm", "pair")


def section_tables(stations):
    a, b = np.arange(RADIX_A), np.arange(RADIX_B)
    angle = ((a[:, None] * a[None, :]) % RADIX_A).astype(np.float32) * np.float32(2.0 * math.pi / RADIX_A)
    cos_a = (np.cos(angle) * np.float32(1.0 / math.sqrt(RADIX_A))).astype(np.float32)
    sin_a = (np.sin(angle) * np.float32(1.0 / math.sqrt(RADIX_A))).astype(np.float32)
    small = np.stack([np.stack([cos_a, sin_a], 1), np.stack([-sin_a, cos_a], 1)], 0)
    first = np.einsum("st,pkrn->psktrn", np.eye(stations, dtype=np.float32), small)
    rows = 2 * stations * RADIX_A
    first = first.reshape(rows, rows)
    turn = (a[:, None] * b[None, :]).astype(np.float32) * np.float32(2.0 * math.pi / NCHAN)
    twist = np.stack([np.cos(turn), np.sin(turn)]).astype(np.float32)
    twist = np.tile(twist, (1, stations, 1))
    angle = ((b[:, None] * b[None, :]) % RADIX_B).astype(np.float32) * np.float32(2.0 * math.pi / RADIX_B)
    cos_b = (np.cos(angle) * np.float32(1.0 / math.sqrt(RADIX_B))).astype(np.float32)
    sin_b = (np.sin(angle) * np.float32(1.0 / math.sqrt(RADIX_B))).astype(np.float32)
    second = np.stack([np.stack([cos_b, -sin_b], 1), np.stack([sin_b, cos_b], 1)], 0)
    second = second.reshape(2, RADIX_B, 2, OUTCH, QUADS).transpose(0, 1, 4, 2, 3)
    second = second.reshape(2 * RADIX_B, 2 * RADIX_B)
    return jnp.asarray(first, BF16), jnp.asarray(twist), jnp.asarray(second, BF16)


def spectra_kernel(dims, delays, own, following, beyond, first, twist, second, phase, out,
                   series, windows, turned, planes, rows):
    frames, stations = dims
    held, ahead, last = own.shape[2], following.shape[2], beyond.shape[2]
    sk = stations * RADIX_A

    def widen(s, carry):
        for r in range(2):
            series[r, s, 0:held] = own[r, s].astype(F32)
            series[r, s, held:held + ahead] = following[r, s].astype(F32)
            series[r, s, held + ahead:held + ahead + last] = beyond[r, s].astype(F32)
            series[r, s, held + ahead + last:] = jnp.zeros((8, LANES), F32)
        return carry

    lax.fori_loop(0, stations, widen, 0)
    lane = lax.broadcasted_iota(jnp.int32, (RADIX_A, LANES), 1)

    def one_frame(f, carry):
        for s in range(stations):
            offset = f * NCHAN + delays[s, f]
            row, shift = offset // LANES, offset % LANES
            for r in range(2):
                parts = [
                    pltpu.roll(series[r, s, pl.ds(row + h, RADIX_A, stride=QUADS), :], (LANES - shift) % LANES, 1)
                    for h in range(QUADS + 1)
                ]
                for h in range(QUADS):
                    cut = jnp.where(lane < LANES - shift, parts[h], parts[h + 1])
                    windows[(2 * s + r) * RADIX_A:(2 * s + r + 1) * RADIX_A, h * LANES:(h + 1) * LANES] = cut.astype(BF16)
        passed = jnp.dot(first[...], windows[...], preferred_element_type=F32)
        real, imag = passed[:sk], passed[sk:]
        here = pl.ds(pl.multiple_of(f * sk, sk), sk)
        turned[here, 0:RADIX_B] = (real * twist[0] + imag * twist[1]).astype(BF16)
        turned[here, RADIX_B:] = (imag * twist[0] - real * twist[1]).astype(BF16)
        return carry

    lax.fori_loop(0, frames, one_frame, 0)
    for g in range(QUADS):
        channels = jnp.dot(turned[...], second[:, g * 2 * LANES:(g + 1) * 2 * LANES], preferred_element_type=F32)
        real = channels[:, :LANES].reshape(frames, sk, LANES)
        imag = channels[:, LANES:].reshape(frames, sk, LANES)
        cosine, sine = phase[0, g], phase[1, g]
        turned_re = (real * cosine - imag * sine).reshape(frames * stations, RADIX_A, LANES)
        turned_im = (real * sine + imag * cosine).reshape(frames * stations, RADIX_A, LANES)
        planes[:, g * RADIX_A:(g + 1) * RADIX_A, :] = turned_re
        planes[:, CHAVG + g * RADIX_A:CHAVG + (g + 1) * RADIX_A, :] = turned_im

    count = frames * stations

    def flip(i, carry):
        rows[pl.ds(i, OUTCH, stride=count), :] = planes[i].T
        return carry

    lax.fori_loop(0, count, flip, 0, unroll=4)
    out[...] = rows[...].astype(BF16).reshape(out.shape)


def product_kernel(dims, bins, assignment, spectra, out, sums):
    owners, pairs, group, slots = dims
    depth, frames = spectra.shape[2], spectra.shape[3]
    pairings = depth // group
    stations = pairs * spectra.shape[4]
    sums[...] = jnp.zeros_like(sums)
    lane = lax.broadcasted_iota(jnp.int32, (stations, LANES), 1)

    def one_owner(t, carry):
        for f in range(frames):
            b = bins[t * frames + f]
            for op in range(pairings):
                grams = []
                for o2 in range(group):
                    held = [spectra[t, p, op * group + o2, f].astype(F32) for p in range(pairs)]
                    left = jnp.concatenate(held, 0)
                    swapped = pltpu.roll(left, CHAVG, 1)
                    swapped = jnp.where(lane < CHAVG, -swapped, swapped)
                    right = jnp.concatenate([left, swapped], 0).astype(BF16)
                    grams.append(lax.dot_general(
                        left.astype(BF16), right, (((1,), (1,)), ((), ())), preferred_element_type=F32))
                if group == 1:
                    grams.append(jnp.zeros_like(grams[0]))
                sums[b, op] += jnp.concatenate(grams, 1)
        return carry

    lax.fori_loop(0, owners, one_owner, 0)
    width = slots * 2 * GROUP_ST
    source = lax.broadcasted_iota(jnp.int32, (LANES, LANES), 0)
    target = lax.broadcasted_iota(jnp.int32, (LANES, LANES), 1)
    slot_of = (target // (2 * GROUP_ST)) % slots
    wanted = (target // width) * (2 * stations) + (target // GROUP_ST) % 2 * stations + target % GROUP_ST
    inside = target < group * width
    total = sums.shape[0] * pairings * GROUP_ST
    for p in range(pairs):
        moved = jnp.zeros((total, LANES), F32)
        for k in range(slots):
            block = assignment[p * slots + k]
            top = pl.multiple_of(block // NGRP * GROUP_ST, GROUP_ST)
            left = block % NGRP * GROUP_ST
            lines = sums[:, :, pl.ds(top, GROUP_ST), :].reshape(total, LANES)
            pick = (source == wanted + left) & (slot_of == k) & inside
            moved += jnp.dot(
                (lines * (1.0 / CHAVG)).astype(BF16),
                jnp.where(pick, 1.0, 0.0).astype(BF16),
                preferred_element_type=F32)
        out[:, p] = moved.reshape(owners, -1, pairings * GROUP_ST, LANES).astype(BF16)


def place_kernel(dims, received, out, lines):
    replicas, depth, group = dims
    count, here, rows_of = received.shape[0], received.shape[1], received.shape[2]
    pairings = rows_of // GROUP_ST
    slots = out.shape[1]
    width = slots * 2 * GROUP_ST
    lines[...] = received[...].reshape(lines.shape).astype(F32)
    row = lax.broadcasted_iota(jnp.int32, (pairings * count, OUTCH), 0)
    lane = lax.broadcasted_iota(jnp.int32, (pairings * count, OUTCH), 1)
    device, op = row % count, row // count
    places = []
    for o2 in range(group):
        channel = device // replicas * depth + op * group + o2
        hit = (channel == lane) & (device % replicas == 0)
        places.append(jnp.where(hit, 1.0, 0.0).astype(BF16))

    def one(step, carry):
        b, p = step // GROUP_ST, step % GROUP_ST
        sent = [
            lines[pl.ds(b * rows_of + op * GROUP_ST + p, count, stride=here * rows_of), :]
            for op in range(pairings)
        ]
        sent = jnp.concatenate(sent, 0)
        value = jnp.zeros((width, OUTCH), F32)
        for o2 in range(group):
            part = sent[:, o2 * width:(o2 + 1) * width].astype(BF16)
            value += lax.dot_general(
                part, places[o2], (((0,), (0,)), ((), ())), preferred_element_type=F32)
        value = value.reshape(slots, 2, GROUP_ST, OUTCH)
        out[b, :, :, pl.ds(pl.multiple_of(p * GROUP_ST, GROUP_ST), GROUP_ST), :] = value
        return carry

    lax.fori_loop(0, here * GROUP_ST, one, 0, unroll=2)


VMEM = pl.BlockSpec(memory_space=pltpu.VMEM)
SMEM = pl.BlockSpec(memory_space=pltpu.SMEM)
PARAMS = pltpu.CompilerParams(vmem_limit_bytes=48 * 1024 * 1024)


def from_behind(value, axis, steps):
    count = lax.axis_size(axis)
    first, last = (max(0, -steps), min(count, count - steps))
    return lax.ppermute(value, axis, [(source, source + steps) for source in range(first, last)])


def exchange(value):
    return lax.all_to_all(value, AXES, split_axis=0, concat_axis=0, tiled=True)


def body(voltages, delays, phase_model, phase_bins, assignment):
    owners, pairs = lax.axis_size("tm"), lax.axis_size("pair")
    devices = owners * pairs
    stations, samples = voltages.shape[1], voltages.shape[2]
    frames = samples // NCHAN
    slots = assignment.shape[0]
    channel_groups = min(devices, OUTCH)
    depth = OUTCH // channel_groups
    replicas = devices // channel_groups
    group = min(2, depth)
    count = frames * stations

    first, twist, second = section_tables(stations)
    lines = voltages.reshape(2, stations, samples // LANES, LANES)
    ahead = min(DELAY_MAX, samples)
    last = DELAY_MAX - ahead
    following = from_behind(lines[:, :, :ahead // LANES], "tm", -1)
    beyond = from_behind(lines[:, :, :last // LANES], "tm", -2)

    every_bin = lax.all_gather(phase_bins, "tm", axis=0, tiled=True)
    every_slot = lax.all_gather(assignment, "pair", axis=0, tiled=True)

    angles = lax.dynamic_slice_in_dim(phase_model, lax.axis_index("pair") * stations, stations, 0)
    angles = angles.reshape(stations, OUTCH, QUADS, RADIX_A).transpose(2, 0, 3, 1)
    angles = angles.reshape(QUADS, stations * RADIX_A, OUTCH)
    phase = jnp.stack([jnp.cos(angles), jnp.sin(angles)])

    total_rows = (samples + DELAY_MAX) // LANES + 8
    sk = stations * RADIX_A
    spectra = pl.pallas_call(
        functools.partial(spectra_kernel, (frames, stations)),
        out_shape=jax.ShapeDtypeStruct((OUTCH, count, LANES), BF16),
        in_specs=[SMEM] + [VMEM] * 7,
        out_specs=VMEM,
        scratch_shapes=[
            pltpu.VMEM((2, stations, total_rows, LANES), F32),
            pltpu.VMEM((2 * sk, RADIX_B), BF16),
            pltpu.VMEM((frames * sk, 2 * RADIX_B), BF16),
            pltpu.VMEM((count, LANES, LANES), F32),
            pltpu.VMEM((OUTCH * count, LANES), F32),
        ],
        compiler_params=PARAMS,
        name="spectra",
    )(delays, lines, following, beyond, first, twist, second, phase)

    sent = spectra.reshape(channel_groups, depth * count, LANES)
    if replicas > 1:
        sent = jnp.repeat(sent, replicas, axis=0)
    routed = exchange(sent)
    routed = routed.reshape(owners, pairs, depth, frames, stations, LANES)

    all_bins = BINS
    bins_here = all_bins // owners
    rows_of = depth // group * GROUP_ST
    binned = pl.pallas_call(
        functools.partial(product_kernel, (owners, pairs, group, slots)),
        out_shape=jax.ShapeDtypeStruct((owners, pairs, bins_here, rows_of, LANES), BF16),
        in_specs=[SMEM, SMEM, VMEM],
        out_specs=VMEM,
        scratch_shapes=[pltpu.VMEM((all_bins, depth // group, pairs * stations, LANES), F32)],
        compiler_params=PARAMS,
        name="products",
    )(every_bin, every_slot, routed)

    returned = exchange(binned.reshape(devices, bins_here, rows_of, LANES))
    return pl.pallas_call(
        functools.partial(place_kernel, (replicas, depth, group)),
        out_shape=jax.ShapeDtypeStruct((bins_here, slots, 2, GROUP_ST * GROUP_ST, OUTCH), F32),
        in_specs=[VMEM],
        out_specs=VMEM,
        scratch_shapes=[pltpu.VMEM((devices * bins_here * rows_of, LANES), F32)],
        compiler_params=PARAMS,
        name="place",
    )(returned)


def solution(mesh):
    in_specs = (P(None, "pair", "tm"), P("pair", "tm"), P(), P("tm"), P("pair"))
    out_specs = P("tm", "pair", None, None, None)
    return jax.shard_map(body, mesh=mesh, in_specs=in_specs, out_specs=out_specs, check_vma=False)
```

time: 636 us -> 114 us (0.18); the launches traced: 625 us -> 114 us
  local copies, waits for them, and re-layouts: 238 us -> 16 us
  matrix products: 184 us -> 0 us
  waiting for transfers between devices: 83.4 us -> 24 us
  other arithmetic: 52.7 us -> 0.98 us
  Pallas kernels: 0 us -> 18.2 us
  between operations: 14.6 us -> 1.38 us
    gather x112 -> x0, local copies, waits for them, and re-layouts: 196 us -> none
    dot_general x13 -> x0, matrix products: 184 us -> none  [the longest x4 176 us: slot_products(): jnp.einsum('ifargo,jfasgo->firjso', left_block, right_block, preferred_el...]
    all_gather x4 -> x0, waiting for transfers between devices: 54.7 us -> none  [body(): spectra = lax.all_gather(local_spectra, 'pair', axis=0, tiled=True)]
    add x4 -> x0, other arithmetic: 21.1 us -> none  [slot_products(): real_part = gram_terms[:, :, 0, :, 0] + gram_terms[:, :, 1, :, 1]]
    pallas_call x0 -> x3, Pallas kernels: none -> 18.2 us  [the longest x1 7.91 us: body(): pl.pallas_call(functools.partial(spectra_kernel, (frames, stations)), out...]
    unnamed x1 -> x2, blocking collectives: 13.7 us -> 28.3 us
    transpose x1 -> x0, other arithmetic: 11.9 us -> none  [cut(): return lax.dynamic_slice_in_dim(series, offset, frame_span, 1)]
    all_to_all x1, blocking collectives: 29.2 us -> 18.4 us  [exchange(): return lax.all_to_all(value, AXES, split_axis=0, concat_axis=0, tiled=True)]
  transfers between devices with their start and end apart: 7 -> 3, of which waited for: 6 -> 1; matrix products, arithmetic and copies ran while one was open for 6% -> 14% of each run, Pallas kernels for 0% -> 0%
where the time goes in v1:
time: 114 us
  blocking collectives  46.7 us (41%)
  waiting for transfers between devices  24 us (21%)
  Pallas kernels  18.2 us (16%)
  local copies, waits for them, and re-layouts  16 us (14%)
  starting transfers between devices  6.49 us (6%)
  between operations  1.38 us (1%)
    unnamed x2, blocking collectives  28.3 us
    ppermute x2, waiting for transfers between devices, from_behind(): lax.ppermute(value, axis, [(source, source + steps) for source in range(f...  24 us
    all_to_all x1, blocking collectives, exchange(): return lax.all_to_all(value, AXES, split_axis=0, concat_axis=0, tiled=True)  18.4 us
    pallas_call x1, Pallas kernels, body(): pl.pallas_call(functools.partial(spectra_kernel, (frames, stations)), out...  7.91 us
    cos x3, local copies, waits for them, and re-layouts, body(): phase = jnp.stack([jnp.cos(angles), jnp.sin(angles)])  6.53 us
    pallas_call x1, Pallas kernels, body(): pl.pallas_call(functools.partial(place_kernel, (replicas, depth, group)),...  5.9 us
    sin x2, local copies, waits for them, and re-layouts, body(): phase = jnp.stack([jnp.cos(angles), jnp.sin(angles)])  5.4 us
    pallas_call x1, Pallas kernels, body(): pl.pallas_call(functools.partial(product_kernel, (owners, pairs, group, s...  4.42 us
  transfers between devices with their start and end apart: 3, of which 1 were waited for; matrix products, arithmetic and copies ran while one was open for 14% of the time, Pallas kernels for 0%

profile of v1, /device:TPU:0, one launch (start us, length us, event | category | flops | bytes accessed | tf_op | source)
XLA Modules:
  0.0 113.7 jit_solution(16817621036031039321)
XLA Ops:
  0.0 1.4 %copy.17 = bf16[2,8,256,128]{3,2,1,0:T(8,128)(2,1)S(1)} copy(bf16[2,8,256,128]{3,1,2,0:T(8,128)(2,1)} %bitcast.19) | data formatting | bytes 2097152
  1.4 1.3 %collective-permute-start = (bf16[2,8,256,128]{3,2,1,0:T(8,128)(2,1)S(1)}, bf16[2,8,256,128]{3,2,1,0:T(8,128)(2,1)S(1)}, u32[]{:S(2)}, u32[]{:S(2)}) collective-permute-start(bf16[2,8,256,128]{3,2,1,0:T(8,128)(2,1)S(1)} %copy.17), channel_id=1, source_target_pairs={{4,0},{8,4},{12,8},{16,12},{20,16},{24,20},{28,24},{5,1},{9,5},{13... | collective-permute-start | bytes 3145736 | tf_op jit(solution)/shard_map/ppermute | solution.py:197
  2.7 0.8 slice.4
  3.5 1.3 %collective-permute-start.1 = (bf16[2,8,128,128]{3,2,1,0:T(8,128)(2,1)}, bf16[2,8,128,128]{3,2,1,0:T(8,128)(2,1)S(1)}, u32[]{:S(2)}, u32[]{:S(2)}) collective-permute-start(bf16[2,8,128,128]{3,2,1,0:T(8,128)(2,1)} %slice.4), channel_id=1, source_target_pairs={{8,0},{12,4},{16,8},{20,12},{24,16},{28,20},{9,1},{13,5},{17,9},{2... | collective-permute-start | bytes 1572872 | tf_op jit(solution)/shard_map/ppermute | solution.py:197
  4.8 1.9 %dynamic-slice_cosine_fusion = (f32[8,8192]{1,0:T(8,128)S(1)}, f32[8,8192]{1,0:T(8,128)S(1)}) fusion(f32[32,8192]{1,0:T(8,128)} %param.10, s32[]{:T(128)S(6)} %select_n.3), kind=kLoop, calls=%fused_computation.3 | loop fusion | bytes 786436 | tf_op jit(solution)/shard_map/cos | solution.py:229
  6.7 2.8 %cos.20 = f32[8,128,4,16]{3,2,1,0:T(4,128)} reshape(f32[8,8192]{1,0:T(8,128)S(1)} %get-tuple-element.5) | data formatting | bytes 524288 | tf_op jit(solution)/shard_map/cos | solution.py:229
  9.5 1.8 %copy.12 = f32[4,8,16,128]{3,2,1,0:T(8,128)S(1)} copy(f32[4,8,16,128]{2,0,3,1:T(4,128)} %bitcast.17) | data formatting | bytes 524288 | tf_op jit(solution)/shard_map/cos | solution.py:229
  11.4 0.0 copy-start.2
  11.4 2.8 %sin.20 = f32[8,128,4,16]{3,2,1,0:T(4,128)} reshape(f32[8,8192]{1,0:T(8,128)S(1)} %get-tuple-element.6) | data formatting | bytes 524288 | tf_op jit(solution)/shard_map/sin | solution.py:229
  14.2 0.0 copy-start
  14.2 0.0 copy-start.1
  14.2 2.6 %copy.13 = f32[4,8,16,128]{3,2,1,0:T(8,128)} copy(f32[4,8,16,128]{2,0,3,1:T(4,128)} %bitcast.18) | data formatting | bytes 524288 | tf_op jit(solution)/shard_map/sin | solution.py:229
  16.8 0.0 copy-done.2
  16.8 0.1 copy.14.delays
  16.9 1.0 pad_maximum_fusion.phase
  17.9 24.0 %collective-permute-done.1.beyond = bf16[2,8,128,128]{3,2,1,0:T(8,128)(2,1)S(1)} collective-permute-done((bf16[2,8,128,128]{3,2,1,0:T(8,128)(2,1)}, bf16[2,8,128,128]{3,2,1,0:T(8,128)(2,1)S(1)}, u32[]{:S(2)}, u32[]{:S(2)}) %collective-permute-start.1) | collective-permute-done | bytes 524320 | tf_op jit(solution)/shard_map/ppermute | solution.py:197
  41.8 0.0 collective-permute-done.following
  41.8 0.0 copy-done
  41.9 0.0 copy-done.1
  41.9 7.9 %spectra.1 = bf16[128,32,128]{2,1,0:T(8,128)(2,1)} custom-call(s32[8,4]{1,0:T(8,128)S(1)} %copy.14.delays, bf16[2,8,256,128]{3,2,1,0:T(8,128)(2,1)S(1)} %copy.17, bf16[2,8,256,128]{3,2,1,0:T(8,128)(2,1)S(1)} %collective-permute-done.following, bf16[2,8,128,128]{3,2,1,0:T(8,128)(2,1)S(1)} %collective-permute-done.1.beyond, bf16[256,256]{1,0:T(8,128)(2,1)S(1)} %copy-done.1, ...), custom_call_target="tpu_custom_call" | custom-call | tf_op jit(solution)/shard_map/spectra/pallas_call | solution.py:233
  49.8 0.0 copy-start.6
  49.8 0.0 copy-start.5
  49.8 0.0 copy-start.3
  49.8 0.0 copy-start.4
  49.8 3.9 %all-to-all-start = ((bf16[32,128,128]{2,1,0:T(8,128)(2,1)}), bf16[32,128,128]{2,1,0:T(8,128)(2,1)S(1)}, u32[]{:S(2)}, u32[]{:S(2)}) async-start(bf16[32,128,128]{2,1,0:T(8,128)(2,1)} %bitcast.6), calls=%async_computation | async-start | bytes 2097152 | tf_op jit(solution)/shard_map/all_to_all | solution.py:201
  53.7 0.0 copy-done.6
  53.7 0.6 dynamic-slice
  54.3 0.0 copy-done.5
  54.3 0.7 dynamic-slice.1
  56.2 0.0 copy-done.3
  56.2 0.2 dynamic-update-slice
  56.5 0.0 copy-done.4
  56.5 0.2 dynamic-update-slice.1
  56.7 23.4 %all-reduce.bins = s32[32]{0:T(128)S(1)} all-reduce(s32[32]{0:T(128)S(1)} %dynamic-update-slice), channel_id=1, replica_groups=mesh['tm'=8,'pair'=4] {'tm'}, use_global_device_ids=true, to_apply=%add | all-reduce | flops 32 | bytes 256
  80.1 4.9 %all-reduce.1.assignment = s32[16]{0:T(128)S(1)} all-reduce(s32[16]{0:T(128)S(1)} %dynamic-update-slice.1), channel_id=1, replica_groups=mesh['tm'=8,'pair'=4] {'pair'}, use_global_device_ids=true, to_apply=%add.1 | all-reduce | flops 16 | bytes 128
  85.0 0.0 all-to-all-done
  85.0 4.4 %products.1 = bf16[8,4,4,16,128]{4,3,2,1,0:T(8,128)(2,1)S(1)} custom-call(s32[32]{0:T(128)S(1)} %all-reduce.bins, s32[16]{0:T(128)S(1)} %all-reduce.1.assignment, bf16[8,4,4,4,8,128]{5,4,3,2,1,0:T(8,128)(2,1)S(1)} %bitcast.15), custom_call_target="tpu_custom_call" | custom-call | tf_op jit(solution)/shard_map/products/pallas_call | solution.py:258
  89.4 18.4 %all_to_all.10.received = bf16[32,4,16,128]{3,2,1,0:T(8,128)(2,1)S(1)} all-to-all(bf16[32,4,16,128]{3,2,1,0:T(8,128)(2,1)S(1)} %bitcast.16), channel_id=1, replica_groups=mesh['tm'=8,'pair'=4] {'tm','pair'}, dimensions={0} | all-to-all | bytes 1048576 | tf_op jit(solution)/shard_map/all_to_all | solution.py:201
  107.8 5.9 %place.1 = f32[4,4,2,64,128]{4,3,2,1,0:T(8,128)} custom-call(bf16[32,4,16,128]{3,2,1,0:T(8,128)(2,1)S(1)} %all_to_all.10.received), custom_call_target="tpu_custom_call" | custom-call | tf_op jit(solution)/shard_map/place/pallas_call | solution.py:269
  (2 shorter events, 0.0 us)
Async XLA Ops:
  1.4 40.4 %collective-permute-start = (bf16[2,8,256,128]{3,2,1,0:T(8,128)(2,1)S(1)}, bf16[2,8,256,128]{3,2,1,0:T(8,128)(2,1)S(1)}, u32[]{:S(2)}, u32[]{:S(2)}) collective-permute-start(bf16[2,8,256,128]{3,2,1,0:T(8,128)(2,1)S(1)} %copy.17), channel_id=1, source_target_pairs={{4,0},{8,4},{12,8},{16,12},{20,16},{24,20},{28,24},{5,1},{9,5},{13... | collective-permute-start | bytes 3145736 | tf_op jit(solution)/shard_map/ppermute | solution.py:197
  3.5 38.3 %collective-permute-start.1 = (bf16[2,8,128,128]{3,2,1,0:T(8,128)(2,1)}, bf16[2,8,128,128]{3,2,1,0:T(8,128)(2,1)S(1)}, u32[]{:S(2)}, u32[]{:S(2)}) collective-permute-start(bf16[2,8,128,128]{3,2,1,0:T(8,128)(2,1)} %slice.4), channel_id=1, source_target_pairs={{8,0},{12,4},{16,8},{20,12},{24,16},{28,20},{9,1},{13,5},{17,9},{2... | collective-permute-start | bytes 1572872 | tf_op jit(solution)/shard_map/ppermute | solution.py:197
  11.4 5.4 %copy-start.2 = (s32[8,4]{0,1:T(4,128)S(1)}, s32[8,4]{0,1:T(4,128)}, u32[]{:S(2)}) copy-start(s32[8,4]{0,1:T(4,128)} %param.9) | copy-start | bytes 388
  14.2 27.6 %copy-start = (f32[2,128,512]{2,1,0:T(8,128)S(1)}, f32[2,128,512]{2,1,0:T(8,128)}, u32[]{:S(2)}) copy-start(f32[2,128,512]{2,1,0:T(8,128)} %constant.17.clone.twist) | copy-start | bytes 1572868
  14.2 27.6 %copy-start.1 = (bf16[256,256]{1,0:T(8,128)(2,1)S(1)}, bf16[256,256]{1,0:T(8,128)(2,1)}, u32[]{:S(2)}) copy-start(bf16[256,256]{1,0:T(8,128)(2,1)} %constant.16.clone.first) | copy-start | bytes 393220
  49.8 3.9 %copy-start.6 = (u32[32]{0:T(128)S(1)}, u32[32]{0:T(128)}, u32[]{:S(2)}) copy-start(u32[32]{0:T(128)} %constant.23) | copy-start | bytes 388
  49.8 4.5 %copy-start.5 = (u32[32]{0:T(128)S(1)}, u32[32]{0:T(128)}, u32[]{:S(2)}) copy-start(u32[32]{0:T(128)} %constant.28) | copy-start | bytes 388
  49.8 6.5 %copy-start.3 = (s32[4]{0:T(128)S(1)}, s32[4]{0:T(128)}, u32[]{:S(2)}) copy-start(s32[4]{0:T(128)} %param.11) | copy-start | bytes 52
  49.8 6.7 %copy-start.4 = (s32[4]{0:T(128)S(1)}, s32[4]{0:T(128)}, u32[]{:S(2)}) copy-start(s32[4]{0:T(128)} %param.12) | copy-start | bytes 52
  49.8 35.2 %all-to-all-start = ((bf16[32,128,128]{2,1,0:T(8,128)(2,1)}), bf16[32,128,128]{2,1,0:T(8,128)(2,1)S(1)}, u32[]{:S(2)}, u32[]{:S(2)}) async-start(bf16[32,128,128]{2,1,0:T(8,128)(2,1)} %bitcast.6), calls=%async_computation | async-start | bytes 2097152 | tf_op jit(solution)/shard_map/all_to_all | solution.py:201

commit v2 on v1

--- a/solution.py
+++ b/solution.py
@@ -45,7 +45,7 @@
     return jnp.asarray(first, BF16), jnp.asarray(twist), jnp.asarray(second, BF16)
 
 
-def spectra_kernel(dims, delays, own, following, beyond, first, twist, second, phase, out,
+def spectra_kernel(dims, delays, ahead_of, own, following, beyond, first, twist, second, phase, out,
                    series, windows, turned, planes, rows):
     frames, stations = dims
     held, ahead, last = own.shape[2], following.shape[2], beyond.shape[2]
@@ -183,7 +183,7 @@
         out[b, :, :, pl.ds(pl.multiple_of(p * GROUP_ST, GROUP_ST), GROUP_ST), :] = value
         return carry
 
-    lax.fori_loop(0, here * GROUP_ST, one, 0, unroll=2)
+    lax.fori_loop(0, here * GROUP_ST, one, 0, unroll=8)
 
 
 VMEM = pl.BlockSpec(memory_space=pltpu.VMEM)
@@ -197,8 +197,70 @@
     return lax.ppermute(value, axis, [(source, source + steps) for source in range(first, last)])
 
 
-def exchange(value):
-    return lax.all_to_all(value, AXES, split_axis=0, concat_axis=0, tiled=True)
+def exchange_kernel(dims, sent, received, send_sems, recv_sems, own_sem):
+    owners, pairs = dims
+    devices = owners * pairs
+    me = lax.axis_index("tm") * pairs + lax.axis_index("pair")
+    barrier = pltpu.get_barrier_semaphore()
+
+    def place_of(device):
+        return (device // pairs, device % pairs)
+
+    def greet(step, carry):
+        peer = (me + step) % devices
+        pl.semaphore_signal(barrier, inc=1, device_id=place_of(peer), device_id_type=pl.DeviceIdType.MESH)
+        return carry
+
+    lax.fori_loop(1, devices, greet, 0)
+    pl.semaphore_wait(barrier, devices - 1)
+
+    def copy_to(step):
+        peer = (me + step) % devices
+        return pltpu.make_async_remote_copy(
+            src_ref=sent.at[peer], dst_ref=received.at[me],
+            send_sem=send_sems.at[step], recv_sem=recv_sems.at[step],
+            device_id=place_of(peer), device_id_type=pl.DeviceIdType.MESH)
+
+    def copy_from(step):
+        peer = (me + devices - step) % devices
+        return pltpu.make_async_remote_copy(
+            src_ref=sent.at[peer], dst_ref=received.at[peer],
+            send_sem=send_sems.at[step], recv_sem=recv_sems.at[step],
+            device_id=place_of(peer), device_id_type=pl.DeviceIdType.MESH)
+
+    def start(step, carry):
+        copy_to(step).start()
+        return carry
+
+    lax.fori_loop(1, devices, start, 0)
+    own = pltpu.make_async_copy(sent.at[me], received.at[me], own_sem)
+    own.start()
+    own.wait()
+
+    def finish(step, carry):
+        copy_to(step).wait_send()
+        copy_from(step).wait_recv()
+        return carry
+
+    lax.fori_loop(1, devices, finish, 0)
+
+
+def exchange(value, number):
+    owners, pairs = lax.axis_size("tm"), lax.axis_size("pair")
+    devices = owners * pairs
+    return pl.pallas_call(
+        functools.partial(exchange_kernel, (owners, pairs)),
+        out_shape=jax.ShapeDtypeStruct(value.shape, value.dtype),
+        in_specs=[VMEM],
+        out_specs=VMEM,
+        scratch_shapes=[
+            pltpu.SemaphoreType.DMA((devices,)),
+            pltpu.SemaphoreType.DMA((devices,)),
+            pltpu.SemaphoreType.DMA,
+        ],
+        compiler_params=pltpu.CompilerParams(collective_id=number, has_side_effects=True),
+        name="exchange",
+    )(value)
 
 
 def body(voltages, delays, phase_model, phase_bins, assignment):
@@ -220,8 +282,10 @@
     following = from_behind(lines[:, :, :ahead // LANES], "tm", -1)
     beyond = from_behind(lines[:, :, :last // LANES], "tm", -2)
 
-    every_bin = lax.all_gather(phase_bins, "tm", axis=0, tiled=True)
-    every_slot = lax.all_gather(assignment, "pair", axis=0, tiled=True)
+    small = lax.all_gather(jnp.concatenate([phase_bins, assignment]), AXES, axis=0)
+    small = small.reshape(owners, pairs, -1)
+    every_bin = small[:, 0, :frames].reshape(-1)
+    every_slot = small[0, :, frames:].reshape(-1)
 
     angles = lax.dynamic_slice_in_dim(phase_model, lax.axis_index("pair") * stations, stations, 0)
     angles = angles.reshape(stations, OUTCH, QUADS, RADIX_A).transpose(2, 0, 3, 1)
@@ -233,7 +297,7 @@
     spectra = pl.pallas_call(
         functools.partial(spectra_kernel, (frames, stations)),
         out_shape=jax.ShapeDtypeStruct((OUTCH, count, LANES), BF16),
-        in_specs=[SMEM] + [VMEM] * 7,
+        in_specs=[SMEM, SMEM] + [VMEM] * 7,
         out_specs=VMEM,
         scratch_shapes=[
             pltpu.VMEM((2, stations, total_rows, LANES), F32),
@@ -244,12 +308,12 @@
         ],
         compiler_params=PARAMS,
         name="spectra",
-    )(delays, lines, following, beyond, first, twist, second, phase)
+    )(delays, every_bin, lines, following, beyond, first, twist, second, phase)
 
     sent = spectra.reshape(channel_groups, depth * count, LANES)
     if replicas > 1:
         sent = jnp.repeat(sent, replicas, axis=0)
-    routed = exchange(sent)
+    routed = exchange(sent, 0)
     routed = routed.reshape(owners, pairs, depth, frames, stations, LANES)
 
     all_bins = BINS
@@ -265,7 +329,7 @@
         name="products",
     )(every_bin, every_slot, routed)
 
-    returned = exchange(binned.reshape(devices, bins_here, rows_of, LANES))
+    returned = exchange(binned.reshape(devices, bins_here, rows_of, LANES), 1)
     return pl.pallas_call(
         functools.partial(place_kernel, (replicas, depth, group)),
         out_shape=jax.ShapeDtypeStruct((bins_here, slots, 2, GROUP_ST * GROUP_ST, OUTCH), F32),

time: 114 us -> 137 us (1.20); the launches traced: 114 us -> 134 us
  Pallas kernels: 18.2 us -> 60.5 us
  waiting for transfers between devices: 24 us -> 0.01 us
  local copies, waits for them, and re-layouts: 16 us -> 22.5 us
  starting transfers between devices: 6.49 us -> 2.57 us
    pallas_call x0 -> x2, Pallas kernels: none -> 46.3 us  [exchange(): pl.pallas_call(functools.partial(exchange_kernel, (owners, pairs)), out_s...]
    ppermute x2, waiting for transfers between devices: 24 us -> 0.01 us  [from_behind(): lax.ppermute(value, axis, [(source, source + steps) for source in range(f...]
    unnamed x2 -> x1, blocking collectives: 28.3 us -> 47.2 us
    all_to_all x1 -> x0, blocking collectives: 18.4 us -> none  [exchange(): return lax.all_to_all(value, AXES, split_axis=0, concat_axis=0, tiled=True)]
    all_to_all x1 -> x0, starting transfers between devices: 3.92 us -> none  [exchange(): return lax.all_to_all(value, AXES, split_axis=0, concat_axis=0, tiled=True)]
    pallas_call x1, Pallas kernels: 5.9 us -> 2.91 us  [body(): pl.pallas_call(functools.partial(place_kernel, (replicas, depth, group)),...]
    unnamed x22 -> x19, local copies, waits for them, and re-layouts: 3.22 us -> 6.19 us
    another operation x0 -> x2, local copies, waits for them, and re-layouts: none -> 1.52 us  [the longest x1 0.76 us: body(): every_slot = small[0, :, frames:].reshape(-1)]
  transfers between devices with their start and end apart: 3 -> 2, of which waited for: 1 -> 0; matrix products, arithmetic and copies ran while one was open for 14% -> 14% of each run, Pallas kernels for 0% -> 0%
where the time goes in v2:
time: 137 us; the launch traced here: 134 us
  Pallas kernels  60.5 us (44%)
  blocking collectives  47.2 us (34%)
  local copies, waits for them, and re-layouts  22.5 us (16%)
  starting transfers between devices  2.57 us (2%)
    unnamed x1, blocking collectives  47.2 us
    pallas_call x2, Pallas kernels, exchange(): pl.pallas_call(functools.partial(exchange_kernel, (owners, pairs)), out_s...  46.3 us
    pallas_call x1, Pallas kernels, body(): pl.pallas_call(functools.partial(spectra_kernel, (frames, stations)), out...  6.94 us
    cos x3, local copies, waits for them, and re-layouts, body(): phase = jnp.stack([jnp.cos(angles), jnp.sin(angles)])  6.52 us
    unnamed x19, local copies, waits for them, and re-layouts  6.19 us
    sin x2, local copies, waits for them, and re-layouts, body(): phase = jnp.stack([jnp.cos(angles), jnp.sin(angles)])  5.37 us
    pallas_call x1, Pallas kernels, body(): pl.pallas_call(functools.partial(product_kernel, (owners, pairs, group, s...  4.42 us
    pallas_call x1, Pallas kernels, body(): pl.pallas_call(functools.partial(place_kernel, (replicas, depth, group)),...  2.91 us
  transfers between devices with their start and end apart: 2, of which 0 were waited for; matrix products, arithmetic and copies ran while one was open for 14% of the time, Pallas kernels for 0%

profile of v2, /device:TPU:0, one launch (start us, length us, event | category | flops | bytes accessed | tf_op | source)
XLA Modules:
  0.0 134.1 jit_solution(649877681822161200)
XLA Ops:
  0.0 1.4 %copy.17 = bf16[2,8,256,128]{3,2,1,0:T(8,128)(2,1)S(1)} copy(bf16[2,8,256,128]{3,1,2,0:T(8,128)(2,1)} %bitcast.18) | data formatting | bytes 2097152
  1.4 1.3 collective-permute-start
  2.7 0.8 slice.14
  3.5 1.3 collective-permute-start.1
  4.8 1.9 %dynamic-slice_cosine_fusion = (f32[8,8192]{1,0:T(8,128)S(1)}, f32[8,8192]{1,0:T(8,128)S(1)}) fusion(f32[32,8192]{1,0:T(8,128)} %param.10, s32[]{:T(128)S(6)} %select_n.3), kind=kLoop, calls=%fused_computation.3 | loop fusion | bytes 786436 | tf_op jit(solution)/shard_map/cos | solution.py:293
  6.7 2.8 %cos.20 = f32[8,128,4,16]{3,2,1,0:T(4,128)} reshape(f32[8,8192]{1,0:T(8,128)S(1)} %get-tuple-element.5) | data formatting | bytes 524288 | tf_op jit(solution)/shard_map/cos | solution.py:293
  9.5 1.8 %copy.12 = f32[4,8,16,128]{3,2,1,0:T(8,128)S(1)} copy(f32[4,8,16,128]{2,0,3,1:T(4,128)} %bitcast.16) | data formatting | bytes 524288 | tf_op jit(solution)/shard_map/cos | solution.py:293
  11.4 0.0 copy-start.6
  11.4 0.0 copy-start.7
  11.4 2.8 %sin.20 = f32[8,128,4,16]{3,2,1,0:T(4,128)} reshape(f32[8,8192]{1,0:T(8,128)S(1)} %get-tuple-element.6) | data formatting | bytes 524288 | tf_op jit(solution)/shard_map/sin | solution.py:293
  14.2 0.0 copy-start.4
  14.2 0.0 copy-start.5
  14.2 2.5 %copy.13 = f32[4,8,16,128]{3,2,1,0:T(8,128)} copy(f32[4,8,16,128]{2,0,3,1:T(4,128)} %bitcast.17) | data formatting | bytes 524288 | tf_op jit(solution)/shard_map/sin | solution.py:293
  16.8 0.0 copy-done.6
  16.8 0.0 copy-done.7
  16.8 0.2 add_dynamic-update-slice_fusion
  16.9 47.2 %all-reduce = s32[256]{0:T(256)} all-reduce(s32[256]{0:T(256)S(1)} %add_dynamic-update-slice_fusion), channel_id=2, replica_groups=mesh['tm'=8,'pair'=4] {'tm','pair'}, use_global_device_ids=true, to_apply=%add | all-reduce | flops 256 | bytes 2048
  64.2 0.8 reshape.41
  65.0 0.7 slice.13
  65.6 0.6 slice_reduce_fusion
  66.2 0.8 reshape_squeeze.6.ahead_of.bins
  67.0 0.8 copy.14.delays
  67.7 0.8 reshape_squeeze.7.assignment
  68.5 1.0 pad_maximum_fusion.phase
  69.5 0.0 collective-permute-done.1.beyond
  69.5 0.0 collective-permute-done.following
  69.5 0.0 copy-done.4
  69.5 0.0 copy-done.5
  69.5 6.9 %spectra.1 = bf16[128,32,128]{2,1,0:T(8,128)(2,1)S(1)} custom-call(s32[8,4]{1,0:T(8,128)S(1)} %copy.14.delays, s32[32]{0:T(128)S(1)} %reshape_squeeze.6.ahead_of.bins, bf16[2,8,256,128]{3,2,1,0:T(8,128)(2,1)S(1)} %copy.17, bf16[2,8,256,128]{3,2,1,0:T(8,128)(2,1)S(1)} %collective-permute-done.following, ...), custom_call_target="tpu_custom_call" | custom-call | tf_op jit(solution)/shard_map/spectra/pallas_call | solution.py:297
  76.5 0.0 copy-start
  76.5 1.0 copy-done
  77.5 23.8 %exchange.2 = bf16[32,128,128]{2,1,0:T(8,128)(2,1)} custom-call(bf16[32,128,128]{2,1,0:T(8,128)(2,1)} %bitcast.13), custom_call_target="tpu_custom_call" | custom-call | tf_op jit(solution)/shard_map/exchange/pallas_call | solution.py:251
  101.2 0.0 copy-start.1
  101.2 1.2 copy-done.1
  102.5 4.4 %products.1 = bf16[8,4,4,16,128]{4,3,2,1,0:T(8,128)(2,1)S(1)} custom-call(s32[32]{0:T(128)S(1)} %reshape_squeeze.6.ahead_of.bins, s32[16]{0:T(128)S(1)} %reshape_squeeze.7.assignment, bf16[8,4,4,4,8,128]{5,4,3,2,1,0:T(8,128)(2,1)S(1)} %bitcast.14), custom_call_target="tpu_custom_call" | custom-call | tf_op jit(solution)/shard_map/products/pallas_call | solution.py:322
  106.9 0.0 copy-start.3
  106.9 0.8 copy-done.3
  107.7 22.5 %exchange.3.received = bf16[32,4,16,128]{3,2,1,0:T(8,128)(2,1)} custom-call(bf16[32,4,16,128]{3,2,1,0:T(8,128)(2,1)} %bitcast.15), custom_call_target="tpu_custom_call" | custom-call | tf_op jit(solution)/shard_map/exchange/pallas_call | solution.py:251
  130.2 0.0 copy-start.2
  130.2 1.0 copy-done.2
  131.2 2.9 %place.1 = f32[4,4,2,64,128]{4,3,2,1,0:T(8,128)} custom-call(bf16[32,4,16,128]{3,2,1,0:T(8,128)(2,1)S(1)} %copy-done.2), custom_call_target="tpu_custom_call" | custom-call | tf_op jit(solution)/shard_map/place/pallas_call | solution.py:333
  (1 shorter events, 0.0 us)
Async XLA Ops:
  1.4 68.1 %collective-permute-start = (bf16[2,8,256,128]{3,2,1,0:T(8,128)(2,1)S(1)}, bf16[2,8,256,128]{3,2,1,0:T(8,128)(2,1)S(1)}, u32[]{:S(2)}, u32[]{:S(2)}) collective-permute-start(bf16[2,8,256,128]{3,2,1,0:T(8,128)(2,1)S(1)} %copy.17), channel_id=1, source_target_pairs={{4,0},{8,4},{12,8},{16,12},{20,16},{24,20},{28,24},{5,1},{9,5},{13... | collective-permute-start | bytes 3145736 | tf_op jit(solution)/shard_map/ppermute | solution.py:197
  3.5 66.0 %collective-permute-start.1 = (bf16[2,8,128,128]{3,2,1,0:T(8,128)(2,1)}, bf16[2,8,128,128]{3,2,1,0:T(8,128)(2,1)S(1)}, u32[]{:S(2)}, u32[]{:S(2)}) collective-permute-start(bf16[2,8,128,128]{3,2,1,0:T(8,128)(2,1)} %slice.14), channel_id=1, source_target_pairs={{8,0},{12,4},{16,8},{20,12},{24,16},{28,20},{9,1},{13,5},{17,9},{2... | collective-permute-start | bytes 1572872 | tf_op jit(solution)/shard_map/ppermute | solution.py:197
  11.4 5.4 %copy-start.6 = (s32[4]{0:T(128)S(1)}, s32[4]{0:T(128)}, u32[]{:S(2)}) copy-start(s32[4]{0:T(128)} %param.12) | copy-start | bytes 52
  11.4 5.4 %copy-start.7 = (s32[4]{0:T(128)S(1)}, s32[4]{0:T(128)}, u32[]{:S(2)}) copy-start(s32[4]{0:T(128)} %param.11) | copy-start | bytes 52
  14.2 55.3 %copy-start.4 = (f32[2,128,512]{2,1,0:T(8,128)S(1)}, f32[2,128,512]{2,1,0:T(8,128)}, u32[]{:S(2)}) copy-start(f32[2,128,512]{2,1,0:T(8,128)} %constant.17.clone.twist) | copy-start | bytes 1572868
  14.2 55.3 %copy-start.5 = (bf16[256,256]{1,0:T(8,128)(2,1)S(1)}, bf16[256,256]{1,0:T(8,128)(2,1)}, u32[]{:S(2)}) copy-start(bf16[256,256]{1,0:T(8,128)(2,1)} %constant.16.clone.first) | copy-start | bytes 393220
  76.5 1.0 copy-start
  101.2 1.2 copy-start.1
  106.9 0.8 copy-start.3
  130.2 1.0 copy-start.2

commit v3 on v1

--- a/solution.py
+++ b/solution.py
@@ -102,7 +102,7 @@
     out[...] = rows[...].astype(BF16).reshape(out.shape)
 
 
-def product_kernel(dims, bins, assignment, spectra, out, sums):
+def product_kernel(dims, small, spectra, out, sums):
     owners, pairs, group, slots = dims
     depth, frames = spectra.shape[2], spectra.shape[3]
     pairings = depth // group
@@ -112,7 +112,7 @@
 
     def one_owner(t, carry):
         for f in range(frames):
-            b = bins[t * frames + f]
+            b = small[t * pairs, f]
             for op in range(pairings):
                 grams = []
                 for o2 in range(group):
@@ -139,7 +139,7 @@
     for p in range(pairs):
         moved = jnp.zeros((total, LANES), F32)
         for k in range(slots):
-            block = assignment[p * slots + k]
+            block = small[p, frames + k]
             top = pl.multiple_of(block // NGRP * GROUP_ST, GROUP_ST)
             left = block % NGRP * GROUP_ST
             lines = sums[:, :, pl.ds(top, GROUP_ST), :].reshape(total, LANES)
@@ -183,7 +183,7 @@
         out[b, :, :, pl.ds(pl.multiple_of(p * GROUP_ST, GROUP_ST), GROUP_ST), :] = value
         return carry
 
-    lax.fori_loop(0, here * GROUP_ST, one, 0, unroll=2)
+    lax.fori_loop(0, here * GROUP_ST, one, 0, unroll=8)
 
 
 VMEM = pl.BlockSpec(memory_space=pltpu.VMEM)
@@ -197,8 +197,82 @@
     return lax.ppermute(value, axis, [(source, source + steps) for source in range(first, last)])
 
 
-def exchange(value):
-    return lax.all_to_all(value, AXES, split_axis=0, concat_axis=0, tiled=True)
+def exchange_kernel(dims, shared, *refs):
+    owners, pairs = dims
+    devices = owners * pairs
+    buffers = 2 if shared else 1
+    sources, targets = refs[:buffers], refs[buffers:2 * buffers]
+    send_sems, recv_sems, own_sems = refs[2 * buffers:]
+    me = lax.axis_index("tm") * pairs + lax.axis_index("pair")
+    barrier = pltpu.get_barrier_semaphore()
+
+    def place_of(device):
+        return (device // pairs, device % pairs)
+
+    def greet(step, carry):
+        peer = (me + step) % devices
+        pl.semaphore_signal(barrier, inc=1, device_id=place_of(peer), device_id_type=pl.DeviceIdType.MESH)
+        return carry
+
+    lax.fori_loop(1, devices, greet, 0)
+    pl.semaphore_wait(barrier, devices - 1)
+
+    def piece(which, device):
+        return sources[0].at[device] if which == 0 else sources[1]
+
+    def copies(step, peer, slot):
+        return [
+            pltpu.make_async_remote_copy(
+                src_ref=piece(which, peer), dst_ref=targets[which].at[slot],
+                send_sem=send_sems.at[which, step], recv_sem=recv_sems.at[which, step],
+                device_id=place_of(peer), device_id_type=pl.DeviceIdType.MESH)
+            for which in range(buffers)
+        ]
+
+    def start(step, carry):
+        for copy in copies(step, (me + step) % devices, me):
+            copy.start()
+        return carry
+
+    lax.fori_loop(1, devices, start, 0)
+    for which in range(buffers):
+        own = pltpu.make_async_copy(piece(which, me), targets[which].at[me], own_sems.at[which])
+        own.start()
+        own.wait()
+
+    def finish(step, carry):
+        for copy in copies(step, (me + step) % devices, me):
+            copy.wait_send()
+        source = (me + devices - step) % devices
+        for copy in copies(step, source, source):
+            copy.wait_recv()
+        return carry
+
+    lax.fori_loop(1, devices, finish, 0)
+
+
+def exchange(value, number, shared=None):
+    owners, pairs = lax.axis_size("tm"), lax.axis_size("pair")
+    devices = owners * pairs
+    shapes = [jax.ShapeDtypeStruct(value.shape, value.dtype)]
+    values = [value]
+    if shared is not None:
+        shapes.append(jax.ShapeDtypeStruct((devices,) + shared.shape, shared.dtype))
+        values.append(shared)
+    result = pl.pallas_call(
+        functools.partial(exchange_kernel, (owners, pairs), shared is not None),
+        out_shape=shapes,
+        in_specs=[VMEM] * len(values),
+        out_specs=[VMEM] * len(values),
+        scratch_shapes=[
+            pltpu.SemaphoreType.DMA((len(values), devices)),
+            pltpu.SemaphoreType.DMA((len(values), devices)),
+            pltpu.SemaphoreType.DMA((len(values),)),
+        ],
+        compiler_params=pltpu.CompilerParams(collective_id=number, has_side_effects=True),
+        name="exchange",
+    )(*values)
+    return result if shared is not None else result[0]
 
 
 def body(voltages, delays, phase_model, phase_bins, assignment):
@@ -219,9 +293,6 @@
     last = DELAY_MAX - ahead
     following = from_behind(lines[:, :, :ahead // LANES], "tm", -1)
     beyond = from_behind(lines[:, :, :last // LANES], "tm", -2)
-
-    every_bin = lax.all_gather(phase_bins, "tm", axis=0, tiled=True)
-    every_slot = lax.all_gather(assignment, "pair", axis=0, tiled=True)
 
     angles = lax.dynamic_slice_in_dim(phase_model, lax.axis_index("pair") * stations, stations, 0)
     angles = angles.reshape(stations, OUTCH, QUADS, RADIX_A).transpose(2, 0, 3, 1)
@@ -249,7 +320,10 @@
     sent = spectra.reshape(channel_groups, depth * count, LANES)
     if replicas > 1:
         sent = jnp.repeat(sent, replicas, axis=0)
-    routed = exchange(sent)
+    own_small = jnp.concatenate([phase_bins, assignment])
+    own_small = jnp.pad(own_small, (0, LANES - own_small.shape[0])).reshape(1, LANES)
+    routed, small = exchange(sent, 0, own_small)
+    small = small[:, 0, :frames + slots]
     routed = routed.reshape(owners, pairs, depth, frames, stations, LANES)
 
     all_bins = BINS
@@ -258,14 +332,14 @@
     binned = pl.pallas_call(
         functools.partial(product_kernel, (owners, pairs, group, slots)),
         out_shape=jax.ShapeDtypeStruct((owners, pairs, bins_here, rows_of, LANES), BF16),
-        in_specs=[SMEM, SMEM, VMEM],
+        in_specs=[SMEM, VMEM],
         out_specs=VMEM,
         scratch_shapes=[pltpu.VMEM((all_bins, depth // group, pairs * stations, LANES), F32)],
         compiler_params=PARAMS,
         name="products",
-    )(every_bin, every_slot, routed)
-
-    returned = exchange(binned.reshape(devices, bins_here, rows_of, LANES))
+    )(small, routed)
+
+    returned = exchange(binned.reshape(devices, bins_here, rows_of, LANES), 1)
     return pl.pallas_call(
         functools.partial(place_kernel, (replicas, depth, group)),
         out_shape=jax.ShapeDtypeStruct((bins_here, slots, 2, GROUP_ST * GROUP_ST, OUTCH), F32),

time: 114 us -> 111 us (0.974); the launches traced: 114 us -> 109 us
  blocking collectives: 46.7 us -> 0 us
  Pallas kernels: 18.2 us -> 62.1 us
  starting transfers between devices: 6.49 us -> 2.57 us
  local copies, waits for them, and re-layouts: 16 us -> 19.5 us
  between operations: 1.38 us -> 0.14 us
    pallas_call x0 -> x2, Pallas kernels: none -> 47.6 us  [exchange(): pl.pallas_call(functools.partial(exchange_kernel, (owners, pairs), shared...]
    unnamed x2 -> x0, blocking collectives: 28.3 us -> none
    all_to_all x1 -> x0, blocking collectives: 18.4 us -> none  [exchange(): return lax.all_to_all(value, AXES, split_axis=0, concat_axis=0, tiled=True)]
    all_to_all x1 -> x0, starting transfers between devices: 3.92 us -> none  [exchange(): return lax.all_to_all(value, AXES, split_axis=0, concat_axis=0, tiled=True)]
    pallas_call x1, Pallas kernels: 5.9 us -> 2.92 us  [body(): pl.pallas_call(functools.partial(place_kernel, (replicas, depth, group)),...]
    unnamed x22 -> x20, local copies, waits for them, and re-layouts: 3.22 us -> 5.52 us
  transfers between devices with their start and end apart: 3 -> 2, of which waited for: 1 -> 1; matrix products, arithmetic and copies ran while one was open for 14% -> 13% of each run, Pallas kernels for 0% -> 0%
where the time goes in v3:
time: 111 us; the launch traced here: 109 us
  Pallas kernels  62.1 us (56%)
  waiting for transfers between devices  23.4 us (21%)
  local copies, waits for them, and re-layouts  19.5 us (18%)
  starting transfers between devices  2.57 us (2%)
    pallas_call x2, Pallas kernels, exchange(): pl.pallas_call(functools.partial(exchange_kernel, (owners, pairs), shared...  47.6 us
    ppermute x2, waiting for transfers between devices, from_behind(): lax.ppermute(value, axis, [(source, source + steps) for source in range(f...  23.4 us
    pallas_call x1, Pallas kernels, body(): pl.pallas_call(functools.partial(spectra_kernel, (frames, stations)), out...  6.93 us
    cos x3, local copies, waits for them, and re-layouts, body(): phase = jnp.stack([jnp.cos(angles), jnp.sin(angles)])  6.51 us
    unnamed x20, local copies, waits for them, and re-layouts  5.52 us
    sin x2, local copies, waits for them, and re-layouts, body(): phase = jnp.stack([jnp.cos(angles), jnp.sin(angles)])  5.38 us
    pallas_call x1, Pallas kernels, body(): pl.pallas_call(functools.partial(product_kernel, (owners, pairs, group, s...  4.68 us
    pallas_call x1, Pallas kernels, body(): pl.pallas_call(functools.partial(place_kernel, (replicas, depth, group)),...  2.92 us
  transfers between devices with their start and end apart: 2, of which 1 were waited for; matrix products, arithmetic and copies ran while one was open for 13% of the time, Pallas kernels for 0%

profile of v3, /device:TPU:0, one launch (start us, length us, event | category | flops | bytes accessed | tf_op | source)
XLA Modules:
  0.0 108.7 jit_solution(4826311064824540584)
XLA Ops:
  0.0 1.4 %copy.19 = bf16[2,8,256,128]{3,2,1,0:T(8,128)(2,1)S(1)} copy(bf16[2,8,256,128]{3,1,2,0:T(8,128)(2,1)} %bitcast.23) | data formatting | bytes 2097152
  1.4 1.3 %collective-permute-start = (bf16[2,8,256,128]{3,2,1,0:T(8,128)(2,1)S(1)}, bf16[2,8,256,128]{3,2,1,0:T(8,128)(2,1)S(1)}, u32[]{:S(2)}, u32[]{:S(2)}) collective-permute-start(bf16[2,8,256,128]{3,2,1,0:T(8,128)(2,1)S(1)} %copy.19), channel_id=1, source_target_pairs={{4,0},{8,4},{12,8},{16,12},{20,16},{24,20},{28,24},{5,1},{9,5},{13... | collective-permute-start | bytes 3145736 | tf_op jit(solution)/shard_map/ppermute | solution.py:197
  2.7 0.8 slice.8
  3.6 1.3 %collective-permute-start.1 = (bf16[2,8,128,128]{3,2,1,0:T(8,128)(2,1)}, bf16[2,8,128,128]{3,2,1,0:T(8,128)(2,1)S(1)}, u32[]{:S(2)}, u32[]{:S(2)}) collective-permute-start(bf16[2,8,128,128]{3,2,1,0:T(8,128)(2,1)} %slice.8), channel_id=1, source_target_pairs={{8,0},{12,4},{16,8},{20,12},{24,16},{28,20},{9,1},{13,5},{17,9},{2... | collective-permute-start | bytes 1572872 | tf_op jit(solution)/shard_map/ppermute | solution.py:197
  4.8 1.9 %dynamic-slice_cosine_fusion = (f32[8,8192]{1,0:T(8,128)S(1)}, f32[8,8192]{1,0:T(8,128)S(1)}) fusion(f32[32,8192]{1,0:T(8,128)} %param.10, s32[]{:T(128)S(6)} %select_n.3), kind=kLoop, calls=%fused_computation.3 | loop fusion | bytes 786436 | tf_op jit(solution)/shard_map/cos | solution.py:300
  6.7 2.8 %cos.20 = f32[8,128,4,16]{3,2,1,0:T(4,128)} reshape(f32[8,8192]{1,0:T(8,128)S(1)} %get-tuple-element.9) | data formatting | bytes 524288 | tf_op jit(solution)/shard_map/cos | solution.py:300
  9.5 1.8 %copy.13 = f32[4,8,16,128]{3,2,1,0:T(8,128)S(1)} copy(f32[4,8,16,128]{2,0,3,1:T(4,128)} %bitcast.21) | data formatting | bytes 524288 | tf_op jit(solution)/shard_map/cos | solution.py:300
  11.4 0.0 copy-start.6
  11.4 0.0 copy-start.7
  11.4 0.0 copy-start.8
  11.4 2.8 %sin.20 = f32[8,128,4,16]{3,2,1,0:T(4,128)} reshape(f32[8,8192]{1,0:T(8,128)S(1)} %get-tuple-element.10) | data formatting | bytes 524288 | tf_op jit(solution)/shard_map/sin | solution.py:300
  14.2 0.0 copy-start.4
  14.2 0.0 copy-start.5
  14.2 2.6 %copy.14 = f32[4,8,16,128]{3,2,1,0:T(8,128)} copy(f32[4,8,16,128]{2,0,3,1:T(4,128)} %bitcast.22) | data formatting | bytes 524288 | tf_op jit(solution)/shard_map/sin | solution.py:300
  16.8 0.0 copy-done.6
  16.8 0.1 copy.15.delays
  16.9 0.0 copy-done.7
  16.9 0.0 copy-done.8
  16.9 0.1 pad_add_fusion
  16.9 0.5 pad_bitcast_fusion.refs_1_
  17.5 1.0 pad_maximum_fusion.phase
  18.4 23.4 %collective-permute-done.1.beyond = bf16[2,8,128,128]{3,2,1,0:T(8,128)(2,1)S(1)} collective-permute-done((bf16[2,8,128,128]{3,2,1,0:T(8,128)(2,1)}, bf16[2,8,128,128]{3,2,1,0:T(8,128)(2,1)S(1)}, u32[]{:S(2)}, u32[]{:S(2)}) %collective-permute-start.1) | collective-permute-done | bytes 524320 | tf_op jit(solution)/shard_map/ppermute | solution.py:197
  41.8 0.0 collective-permute-done.following
  41.8 0.0 copy-done.4
  41.9 0.0 copy-done.5
  41.9 6.9 %spectra.1 = bf16[128,32,128]{2,1,0:T(8,128)(2,1)S(1)} custom-call(s32[8,4]{1,0:T(8,128)S(1)} %copy.15.delays, bf16[2,8,256,128]{3,2,1,0:T(8,128)(2,1)S(1)} %copy.19, bf16[2,8,256,128]{3,2,1,0:T(8,128)(2,1)S(1)} %collective-permute-done.following, bf16[2,8,128,128]{3,2,1,0:T(8,128)(2,1)S(1)} %collective-permute-done.1.beyond, ...), custom_call_target="tpu_custom_call" | custom-call | tf_op jit(solution)/shard_map/spectra/pallas_call | solution.py:304
  48.8 0.0 copy-start
  48.8 1.0 copy-done
  49.8 24.6 %exchange.2 = (bf16[32,128,128]{2,1,0:T(8,128)(2,1)}, s32[32,1,128]{2,1,0:T(1,128)}) custom-call(bf16[32,128,128]{2,1,0:T(8,128)(2,1)} %bitcast.18, s32[1,128]{1,0:T(1,128)} %pad_bitcast_fusion.refs_1_), custom_call_target="tpu_custom_call" | custom-call | tf_op jit(solution)/shard_map/exchange/pallas_call | solution.py:262
  74.4 0.7 slice_bitcast_fusion.small
  75.1 0.0 copy-start.3
  75.1 1.2 %copy-done.3 = bf16[32,128,128]{2,1,0:T(8,128)(2,1)S(1)} copy-done((bf16[32,128,128]{2,1,0:T(8,128)(2,1)S(1)}, bf16[32,128,128]{2,1,0:T(8,128)(2,1)}, u32[]{:S(2)}) %copy-start.3) | copy-done | bytes 1048600
  76.4 4.7 %products.1 = bf16[8,4,4,16,128]{4,3,2,1,0:T(8,128)(2,1)S(1)} custom-call(s32[32,8]{1,0:T(8,128)S(1)} %slice_bitcast_fusion.small, bf16[8,4,4,4,8,128]{5,4,3,2,1,0:T(8,128)(2,1)S(1)} %bitcast.20), custom_call_target="tpu_custom_call" | custom-call | tf_op jit(solution)/shard_map/products/pallas_call | solution.py:332
  81.0 0.0 copy-start.1
  81.1 0.8 copy-done.1
  81.8 22.9 %exchange.3.received = bf16[32,4,16,128]{3,2,1,0:T(8,128)(2,1)} custom-call(bf16[32,4,16,128]{3,2,1,0:T(8,128)(2,1)} %bitcast.19), custom_call_target="tpu_custom_call" | custom-call | tf_op jit(solution)/shard_map/exchange/pallas_call | solution.py:262
  104.8 0.0 copy-start.2
  104.8 1.0 copy-done.2
  105.8 2.9 %place.1 = f32[4,4,2,64,128]{4,3,2,1,0:T(8,128)} custom-call(bf16[32,4,16,128]{3,2,1,0:T(8,128)(2,1)S(1)} %copy-done.2), custom_call_target="tpu_custom_call" | custom-call | tf_op jit(solution)/shard_map/place/pallas_call | solution.py:343
Async XLA Ops:
  1.4 40.4 %collective-permute-start = (bf16[2,8,256,128]{3,2,1,0:T(8,128)(2,1)S(1)}, bf16[2,8,256,128]{3,2,1,0:T(8,128)(2,1)S(1)}, u32[]{:S(2)}, u32[]{:S(2)}) collective-permute-start(bf16[2,8,256,128]{3,2,1,0:T(8,128)(2,1)S(1)} %copy.19), channel_id=1, source_target_pairs={{4,0},{8,4},{12,8},{16,12},{20,16},{24,20},{28,24},{5,1},{9,5},{13... | collective-permute-start | bytes 3145736 | tf_op jit(solution)/shard_map/ppermute | solution.py:197
  3.6 38.3 %collective-permute-start.1 = (bf16[2,8,128,128]{3,2,1,0:T(8,128)(2,1)}, bf16[2,8,128,128]{3,2,1,0:T(8,128)(2,1)S(1)}, u32[]{:S(2)}, u32[]{:S(2)}) collective-permute-start(bf16[2,8,128,128]{3,2,1,0:T(8,128)(2,1)} %slice.8), channel_id=1, source_target_pairs={{8,0},{12,4},{16,8},{20,12},{24,16},{28,20},{9,1},{13,5},{17,9},{2... | collective-permute-start | bytes 1572872 | tf_op jit(solution)/shard_map/ppermute | solution.py:197
  11.4 5.4 %copy-start.6 = (s32[8,4]{0,1:T(4,128)S(1)}, s32[8,4]{0,1:T(4,128)}, u32[]{:S(2)}) copy-start(s32[8,4]{0,1:T(4,128)} %param.9) | copy-start | bytes 388
  11.4 5.5 %copy-start.7 = (s32[4]{0:T(128)S(1)}, s32[4]{0:T(128)}, u32[]{:S(2)}) copy-start(s32[4]{0:T(128)} %param.12) | copy-start | bytes 52
  11.4 5.5 %copy-start.8 = (s32[4]{0:T(128)S(1)}, s32[4]{0:T(128)}, u32[]{:S(2)}) copy-start(s32[4]{0:T(128)} %param.11) | copy-start | bytes 52
  14.2 27.6 %copy-start.4 = (f32[2,128,512]{2,1,0:T(8,128)S(1)}, f32[2,128,512]{2,1,0:T(8,128)}, u32[]{:S(2)}) copy-start(f32[2,128,512]{2,1,0:T(8,128)} %constant.17.clone.twist) | copy-start | bytes 1572868
  14.2 27.6 %copy-start.5 = (bf16[256,256]{1,0:T(8,128)(2,1)S(1)}, bf16[256,256]{1,0:T(8,128)(2,1)}, u32[]{:S(2)}) copy-start(bf16[256,256]{1,0:T(8,128)(2,1)} %constant.16.clone.first) | copy-start | bytes 393220
  48.8 1.0 copy-start
  75.1 1.2 %copy-start.3 = (bf16[32,128,128]{2,1,0:T(8,128)(2,1)S(1)}, bf16[32,128,128]{2,1,0:T(8,128)(2,1)}, u32[]{:S(2)}) copy-start(bf16[32,128,128]{2,1,0:T(8,128)(2,1)} %get-tuple-element.8) | copy-start | bytes 3145732
  81.0 0.8 copy-start.1
  104.8 1.0 copy-start.2
